TPU v7x, 32 devices: a whole 2x2x4 slice. The times are simulated.
32 devices in a mesh: lat: 8 (over y, x, core), lev: 4 (over z).
Axes of the slice: x: 2, y: 2, z: 4, core: 2. Of those that a mesh axis runs over, the one named last changes fastest.
Arguments:
- fields: float32 [12, 128, 256, 1024], P(None, 'lev', 'lat'), may hold values from -6 to 6
- legendre: bfloat16 [256, 256, 256], P('lat'), as said below
- owner_counts: int32 [8], replicated, may hold values from 1 to 64, 256 in all
Outputs:
- covariance: float32 [512, 128, 128], P('lat', 'lev')
Inputs may be any that keep to these rules, and one draw needn't show every extreme that they name: `owner_counts`: each owner holds 1 to 64 total wavenumbers, the counts sum to 256, and some owner holds exactly 64. legendre[lat, m, n] is zero where n < m.
All inputs are finite; a program needn't handle non-finite values.
Results may differ from a plain program's by a relative error of at most 0.0038.
Values may be sent and summed in bfloat16 or wider, within the bound.
A program may use at most 192 MiB of HBM per device.

v0:
```python
import math
import jax
import jax.numpy as jnp
from jax import lax
from jax.sharding import PartitionSpec as P


def fourier_table(points, modes):
    places = jnp.arange(points, dtype=jnp.int32)
    orders = jnp.arange(modes, dtype=jnp.int32)
    phase = places[:, None] * orders[None, :] % points
    angle = phase.astype(jnp.float32) * (2.0 * math.pi / points)
    factor = points ** (-0.5)
    return jnp.stack([jnp.cos(angle) * factor, -jnp.sin(angle) * factor], axis=2)


def on_device(fields, legendre, owner_counts):
    members, lev_rows, lat_rows, points = fields.shape
    modes = legendre.shape[1]
    lev_count = lax.axis_size("lev")
    owners = owner_counts.shape[0]
    capacity = 2 * modes // owners
    dft_table = fourier_table(points, modes)
    spectra = jnp.einsum("belx,xmc->lmcbe", fields, dft_table, precision=lax.Precision.HIGHEST)
    spectra = spectra.reshape(lat_rows, modes, 2 * members * lev_rows).astype(jnp.bfloat16)
    collected_rows, transform_table_rows = (
        lax.all_to_all(spectra, "lat", split_axis=1, concat_axis=0, tiled=True),
        lax.all_to_all(legendre, "lat", split_axis=1, concat_axis=0, tiled=True),
    )
    wavenumber_rows = jnp.einsum(
        "dez,det->tez", collected_rows, transform_table_rows, preferred_element_type=jnp.float32
    )
    resident_modes = wavenumber_rows.shape[1]
    shaped = wavenumber_rows.reshape(modes, resident_modes, 2, members, lev_rows)
    anomaly = (shaped - jnp.mean(shaped, axis=3, keepdims=True)).astype(jnp.bfloat16)
    anomaly = anomaly.reshape(modes, resident_modes, 2 * members * lev_rows)
    starts = jnp.cumsum(owner_counts) - owner_counts
    offset = jnp.arange(capacity, dtype=jnp.int32)
    active_flag = offset[None, :] < owner_counts[:, None]
    slot_index = jnp.where(active_flag, starts[:, None] + offset[None, :], 0).reshape(-1)
    slotted = jnp.take(anomaly, slot_index, axis=0)
    slotted = jnp.where(active_flag.reshape(-1)[:, None, None], slotted, jnp.zeros_like(slotted))
    slotted = slotted[None]
    received = lax.all_to_all(
        lax.all_to_all(slotted, "lat", split_axis=1, concat_axis=2, tiled=True),
        "lev",
        split_axis=2,
        concat_axis=0,
        tiled=True,
    )
    mode_share = received.shape[2]
    blocks = received.reshape(lev_count, capacity, mode_share, 2 * members, lev_rows)
    partial_value = jnp.einsum(
        "esaql,fsaqk->selfk", blocks, blocks, preferred_element_type=jnp.float32
    )
    partial_value = partial_value.reshape(capacity, lev_count * lev_rows, lev_count * lev_rows)
    summed = lax.psum_scatter(partial_value, "lev", scatter_dimension=1, tiled=True)
    owner = lax.axis_index("lat")
    wavenumber = starts[owner] + offset
    live_count = owner_counts[owner]
    divisor = ((members - 1) * (2 * wavenumber + 2)).astype(jnp.float32)
    scaled = summed / divisor[:, None, None]
    return jnp.where((offset < live_count)[:, None, None], scaled, jnp.zeros_like(scaled))


def solution(mesh):
    return jax.shard_map(
        on_device,
        mesh=mesh,
        in_specs=(P(None, "lev", "lat", None), P("lat", None, None), P()),
        out_specs=P("lat", "lev", None),
        check_vma=False,
    )
```

profile of v0, /device:TPU:0, one launch (start us, length us, event | category | flops | bytes accessed | tf_op | source)
XLA Modules:
  0.0 1535.5 jit_solution(14930532763259418552)
XLA Ops:
  6.5 6.5 copy.18
  13.0 5.2 all-to-all-start.1
  18.2 4.2 negate_multiply_fusion
  22.4 85.2 %fusion.7 = bf16[256,2,12,32,32]{0,4,3,2,1:T(8,128)(2,1)} fusion(f32[12,32,32,1024]{3,2,1,0:T(8,128)} %param.3, f32[1024,256,1]{1,0,2:T(8,128)S(1)} %get-tuple-element.7, f32[1024,256,1]{1,0,2:T(8,128)S(1)} %get-tuple-element.8), kind=kOutput, calls=%fused_computation.11 | convolution fusion | flops 77316227072 | bytes 65011712 | tf_op jit(solution)/shard_map/belx,xmc->lmcbe/dot_general | solution.py:24
  107.6 18.2 %copy.15 = bf16[32,256,768]{2,0,1:T(8,128)(2,1)} copy(bf16[32,256,768]{1,0,2:T(8,128)(2,1)} %bitcast.76) | data formatting | bytes 25165824 | tf_op jit(solution)/shard_map/convert_element_type | solution.py:25
  125.9 5.5 all-to-all-start
  131.9 0.4 copy-done.2
  132.6 4.8 copy.19
  137.4 132.9 %all-to-all-done = bf16[32,256,768]{2,0,1:T(8,128)(2,1)} async-done(((bf16[32,256,768]{2,0,1:T(8,128)(2,1)}), bf16[32,256,768]{2,0,1:T(8,128)(2,1)}, u32[]{:S(2)}, u32[]{:S(2)}) %all-to-all-start) | async-done | bytes 12582944 | tf_op jit(solution)/shard_map/all_to_all | solution.py:27
  270.4 14.1 copy.17
  284.4 20.2 %fusion.5 = f32[32,768,256]{2,1,0:T(8,128)} fusion(bf16[256,32,256]{2,0,1:T(8,128)(2,1)} %bitcast.75, bf16[256,32,768]{2,1,0:T(8,128)(2,1)} %bitcast.71), kind=kOutput, calls=%fused_computation.8 | convolution fusion | flops 3221225472 | bytes 41943040 | tf_op jit(solution)/shard_map/dez,det->tez/dot_general | solution.py:30
  304.6 10.0 reduce_sum.9
  314.7 0.2 broadcast_multiply_fusion
  314.9 15.0 fusion.4
  329.9 16.8 %copy.21 = bf16[256,32,768]{2,1,0:T(8,128)(2,1)} copy(bf16[256,32,768]{0,2,1:T(8,128)(2,1)} %fusion.4) | data formatting | bytes 25165824 | tf_op jit(solution)/shard_map/convert_element_type | solution.py:35
  346.6 20.6 %gather_fusion = bf16[512,32,768]{2,1,0:T(8,128)(2,1)} fusion(bf16[256,32,768]{2,1,0:T(8,128)(2,1)} %copy.21, s32[1024]{0:T(1024)S(1)} %pad_clamp_fusion), kind=kCustom, calls=%fused_computation | custom fusion | bytes 50333696 | tf_op jit(solution)/shard_map/jit(_take)/gather | solution.py:41
  367.2 22.1 %fusion.3 = bf16[1,512,32,768]{3,2,0,1:T(8,128)(2,1)} fusion(bf16[512,32,768]{2,1,0:T(8,128)(2,1)} %gather_fusion, pred[512]{0:T(512)(128)(4,1)S(1)} %compare_and_fusion, pred[512]{0:T(512)(128)(4,1)S(1)} %lt.78), kind=kLoop, calls=%fused_computation.5 | loop fusion | flops 25165824 | bytes 50332672 | tf_op jit(solution)/shard_map/jit(_where)/select_n | solution.py:42
  389.3 278.2 %all_to_all.69 = bf16[1,512,32,768]{3,2,0,1:T(8,128)(2,1)S(1)} all-to-all(bf16[1,512,32,768]{3,2,0,1:T(8,128)(2,1)} %fusion.3), channel_id=1, replica_groups=mesh['lat'=8,'lev'=4] {'lat'}, dimensions={1} | all-to-all | bytes 50331648 | tf_op jit(solution)/shard_map/all_to_all | solution.py:45
  667.5 8.7 copy.23
  676.2 23.2 %copy.24 = bf16[1,64,256,768]{3,1,0,2:T(8,128)(2,1)S(1)} copy(bf16[1,64,256,768]{3,2,1,0:T(8,128)(2,1)} %bitcast.69) | data formatting | bytes 50331648 | tf_op jit(solution)/shard_map/all_to_all | solution.py:45
  699.4 548.4 %all_to_all.70 = bf16[1,64,256,768]{3,1,0,2:T(8,128)(2,1)} all-to-all(bf16[1,64,256,768]{3,1,0,2:T(8,128)(2,1)S(1)} %copy.24), channel_id=1, replica_groups=mesh['lat'=8,'lev'=4] {'lev'}, dimensions={2} | all-to-all | bytes 50331648 | tf_op jit(solution)/shard_map/all_to_all | solution.py:44
  1247.8 23.9 %copy.25 = bf16[1,64,256,768]{3,2,1,0:T(8,128)(2,1)} copy(bf16[1,64,256,768]{3,1,0,2:T(8,128)(2,1)} %all_to_all.70) | data formatting | bytes 50331648 | tf_op jit(solution)/shard_map/all_to_all | solution.py:44
  1271.7 44.6 %copy.26 = bf16[4,1,64,64,768]{3,4,0,2,1:T(8,128)(2,1)} copy(bf16[4,1,64,64,768]{4,3,0,2,1:T(8,128)(2,1)} %bitcast.70) | data formatting | bytes 50331648 | tf_op jit(solution)/shard_map/all_to_all | solution.py:44
  1316.4 50.3 %convolution_bitcast_fusion = f32[64,4,32,4,32]{4,2,3,1,0:T(8,128)} fusion(bf16[4,64,64,24,32,1]{2,4,3,5,0,1:T(8,128)(2,1)} %bitcast.72, bf16[4,64,64,24,32,1]{2,4,3,0,5,1:T(8,128)(2,1)} %bitcast.73), kind=kOutput, calls=%fused_computation.10 | convolution fusion | flops 3221225472 | bytes 54525952 | tf_op jit(solution)/shard_map/esaql,fsaqk->selfk/dot_general | solution.py:53
  1366.6 14.6 copy.27
  1381.3 0.6 dynamic_slice.7
  1381.9 0.6 dynamic_slice.6
  1382.5 0.7 multiply_convert_fusion
  1383.2 0.6 iota_compare_fusion.1
  1383.7 141.1 %reduce-scatter.2.cloned.1.call-done = f32[64,32,128]{0,2,1:T(8,128)} async-done(((f32[64,128,128]{0,2,1:T(8,128)}), f32[64,32,128]{0,2,1:T(8,128)}) %reduce-scatter.2.cloned.1.call-update) | async-done | bytes 1048592 | tf_op jit(solution)/shard_map/reduce_scatter | solution.py:57
  1524.8 1.8 divide_select_fusion
  1526.6 1.8 copy.28
  (20 shorter events, 0.8 us)
Async XLA Ops:
  13.0 112.8 %all-to-all-start.1 = ((bf16[32,256,256]{2,0,1:T(8,128)(2,1)}), bf16[32,256,256]{2,0,1:T(8,128)(2,1)}, u32[]{:S(2)}, u32[]{:S(2)}) async-start(bf16[32,256,256]{2,0,1:T(8,128)(2,1)} %copy.18), calls=%async_computation.1 | async-start | bytes 8388608 | tf_op jit(solution)/shard_map/all_to_all | solution.py:28
  125.8 5.8 copy-start
  125.9 144.5 %all-to-all-start = ((bf16[32,256,768]{2,0,1:T(8,128)(2,1)}), bf16[32,256,768]{2,0,1:T(8,128)(2,1)}, u32[]{:S(2)}, u32[]{:S(2)}) async-start(bf16[32,256,768]{2,0,1:T(8,128)(2,1)} %copy.15), calls=%async_computation | async-start | bytes 25165824 | tf_op jit(solution)/shard_map/all_to_all | solution.py:27
  131.4 1393.5 %reduce-scatter.2.cloned.1.call-start = ((), (), s32[]{:S(2)}) async-start(), calls=%async_computation.5 | async-start | bytes 10485760 | tf_op jit(solution)/shard_map/reduce_scatter | solution.py:57
  131.8 0.5 copy-start.2
  1366.6 14.7 copy-start.3
  1366.6 15.3 copy-start.1
Sparse Core Ops, SparseCore 0:
  1381.4 143.3 reduce-scatter.1
where the time goes:
time: 1540 us
  blocking collectives  827 us (54%)
  waiting for transfers between devices  274 us (18%)
  local copies, waits for them, and re-layouts  200 us (13%)
  matrix products  156 us (10%)
  other arithmetic  54.8 us (4%)
    all_to_all x1, blocking collectives, on_device(): lax.all_to_all(lax.all_to_all(slotted, 'lat', split_axis=1, concat_axis=2...  548 us
    all_to_all x1, blocking collectives, on_device(): lax.all_to_all(slotted, 'lat', split_axis=1, concat_axis=2, tiled=True)  278 us
    reduce_scatter x1, waiting for transfers between devices, on_device(): lax.psum_scatter(partial_value, 'lev', scatter_dimension=1, tiled=True)  141 us
    all_to_all x1, waiting for transfers between devices, on_device(): lax.all_to_all(spectra, 'lat', split_axis=1, concat_axis=0, tiled=True)  133 us
    dot_general x1, matrix products, on_device(): jnp.einsum('belx,xmc->lmcbe', fields, dft_table, precision=lax.Precision....  85.2 us
    all_to_all x2, local copies, waits for them, and re-layouts, on_device(): lax.all_to_all(lax.all_to_all(slotted, 'lat', split_axis=1, concat_axis=2...  68.5 us
    dot_general x1, matrix products, on_device(): jnp.einsum('esaql,fsaqk->selfk', blocks, blocks, preferred_element_type=j...  50.3 us
    all_to_all x2, local copies, waits for them, and re-layouts, on_device(): lax.all_to_all(slotted, 'lat', split_axis=1, concat_axis=2, tiled=True)  31.9 us
  transfers between devices with their start and end apart: 3, of which 2 were waited for; matrix products, arithmetic and copies ran while one was open for 8% of the time, Pallas kernels for 0%

commit v1 on v0

--- a/solution.py
+++ b/solution.py
@@ -24,7 +24,12 @@
     spectra = jnp.einsum("belx,xmc->lmcbe", fields, dft_table, precision=lax.Precision.HIGHEST)
     spectra = spectra.reshape(lat_rows, modes, 2 * members * lev_rows).astype(jnp.bfloat16)
     collected_rows, transform_table_rows = (
-        lax.all_to_all(spectra, "lat", split_axis=1, concat_axis=0, tiled=True),
+        jnp.concatenate(
+            lax.all_to_all(
+                jnp.stack(jnp.split(spectra, lax.axis_size("lat"), axis=1)), "lat", 0, 0
+            ),
+            axis=0,
+        ),
         lax.all_to_all(legendre, "lat", split_axis=1, concat_axis=0, tiled=True),
     )
     wavenumber_rows = jnp.einsum(

time: 1540 us -> 1620 us (1.052)
  local copies, waits for them, and re-layouts: 200 us -> 276 us
    unnamed x9 -> x28, local copies, waits for them, and re-layouts: 6.95 us -> 81.9 us
    split x0 -> x1, local copies, waits for them, and re-layouts: none -> 32.3 us  [on_device(): jnp.split(spectra, lax.axis_size('lat'), axis=1)]
    convert_element_type x1 -> x0, local copies, waits for them, and re-layouts: 18.2 us -> none  [on_device(): spectra.reshape(lat_rows, modes, 2 * members * lev_rows)]
  transfers between devices with their start and end apart: 3 -> 3, of which waited for: 2 -> 2; matrix products, arithmetic and copies ran while one was open for 8% -> 13% of each run, Pallas kernels for 0% -> 0%
where the time goes in v1:
time: 1620 us; the launch traced here: 1610 us
  blocking collectives  826 us (51%)
  local copies, waits for them, and re-layouts  276 us (17%)
  waiting for transfers between devices  274 us (17%)
  matrix products  156 us (10%)
  other arithmetic  54.9 us (3%)
    all_to_all x1, blocking collectives, on_device(): lax.all_to_all(lax.all_to_all(slotted, 'lat', split_axis=1, concat_axis=2...  548 us
    all_to_all x1, blocking collectives, on_device(): lax.all_to_all(slotted, 'lat', split_axis=1, concat_axis=2, tiled=True)  278 us
    reduce_scatter x1, waiting for transfers between devices, on_device(): lax.psum_scatter(partial_value, 'lev', scatter_dimension=1, tiled=True)  141 us
    all_to_all x1, waiting for transfers between devices, on_device(): lax.all_to_all(jnp.stack(jnp.split(spectra, lax.axis_size('lat'), axis=1)...  133 us
    dot_general x1, matrix products, on_device(): jnp.einsum('belx,xmc->lmcbe', fields, dft_table, precision=lax.Precision....  85 us
    unnamed x28, local copies, waits for them, and re-layouts  81.9 us
    all_to_all x2, local copies, waits for them, and re-layouts, on_device(): lax.all_to_all(lax.all_to_all(slotted, 'lat', split_axis=1, concat_axis=2...  68.5 us
    dot_general x1, matrix products, on_device(): jnp.einsum('esaql,fsaqk->selfk', blocks, blocks, preferred_element_type=j...  50.2 us
  transfers between devices with their start and end apart: 3, of which 2 were waited for; matrix products, arithmetic and copies ran while one was open for 13% of the time, Pallas kernels for 0%

profile of v1, /device:TPU:0, one launch (start us, length us, event | category | flops | bytes accessed | tf_op | source)
XLA Modules:
  0.0 1611.3 jit_solution(8057386641509092538)
XLA Ops:
  6.5 6.5 copy.29
  13.1 5.2 all-to-all-start.1
  18.3 4.2 negate_multiply_fusion
  22.4 85.0 %fusion.7 = bf16[256,2,12,32,32]{0,4,3,2,1:T(8,128)(2,1)} fusion(f32[12,32,32,1024]{3,2,1,0:T(8,128)} %param.3, f32[1024,256,1]{1,0,2:T(8,128)S(1)} %get-tuple-element.15, f32[1024,256,1]{1,0,2:T(8,128)S(1)} %get-tuple-element.16), kind=kOutput, calls=%fused_computation.11 | convolution fusion | flops 77316227072 | bytes 65011712 | tf_op jit(solution)/shard_map/belx,xmc->lmcbe/dot_general | solution.py:24
  107.4 32.3 %fusion.19 = (bf16[32,32,768]{1,0,2:T(8,128)(2,1)}, bf16[32,32,768]{1,0,2:T(8,128)(2,1)}, bf16[32,32,768]{1,0,2:T(8,128)(2,1)}, bf16[32,32,768]{1,0,2:T(8,128)(2...) fusion(bf16[32,256,768]{1,0,2:T(8,128)(2,1)} %bitcast.81), kind=kLoop, calls=%fused_computation.47 | loop fusion | bytes 25165824 | tf_op jit(solution)/shard_map/split | solution.py:29
  139.7 7.8 copy.44
  147.4 7.7 copy.45
  155.2 7.7 copy.46
  162.9 7.7 copy.47
  170.6 7.8 copy.48
  178.4 7.7 copy.49
  186.1 6.9 copy.50
  193.0 6.9 copy.51
  200.0 2.8 bitcast_dynamic-update-slice_fusion.7
  215.9 5.5 all-to-all-start
  222.5 4.8 copy.30
  227.3 133.1 %all-to-all-done = bf16[8,32,32,768]{3,2,1,0:T(8,128)(2,1)} async-done(((bf16[8,32,32,768]{3,2,1,0:T(8,128)(2,1)}), bf16[8,32,32,768]{3,2,1,0:T(8,128)(2,1)}, u32[]{:S(2)}, u32[]{:S(2)}) %all-to-all-start) | async-done | bytes 12582944 | tf_op jit(solution)/shard_map/all_to_all | solution.py:28
  360.4 20.6 %fusion.5 = f32[32,768,256]{2,1,0:T(8,128)} fusion(bf16[256,32,256]{2,0,1:T(8,128)(2,1)} %bitcast.88, bf16[256,32,768]{2,1,0:T(8,128)(2,1)} %bitcast.17), kind=kOutput, calls=%fused_computation.8 | convolution fusion | flops 3221225472 | bytes 41943040 | tf_op jit(solution)/shard_map/dez,det->tez/dot_general | solution.py:35
  381.0 10.0 reduce_sum.9
  391.2 14.9 fusion.4
  406.1 16.8 %copy.32 = bf16[256,32,768]{2,1,0:T(8,128)(2,1)} copy(bf16[256,32,768]{0,2,1:T(8,128)(2,1)} %fusion.4) | data formatting | bytes 25165824 | tf_op jit(solution)/shard_map/convert_element_type | solution.py:40
  422.9 20.4 %gather_fusion = bf16[512,32,768]{2,1,0:T(8,128)(2,1)} fusion(bf16[256,32,768]{2,1,0:T(8,128)(2,1)} %copy.32, s32[1024]{0:T(1024)S(1)} %pad_clamp_fusion), kind=kCustom, calls=%fused_computation | custom fusion | bytes 50333696 | tf_op jit(solution)/shard_map/jit(_take)/gather | solution.py:46
  443.3 22.1 %fusion.3 = bf16[1,512,32,768]{3,2,0,1:T(8,128)(2,1)} fusion(bf16[512,32,768]{2,1,0:T(8,128)(2,1)} %gather_fusion, pred[512]{0:T(512)(128)(4,1)S(1)} %compare_and_fusion, pred[512]{0:T(512)(128)(4,1)S(1)} %lt.78), kind=kLoop, calls=%fused_computation.5 | loop fusion | flops 25165824 | bytes 50332672 | tf_op jit(solution)/shard_map/jit(_where)/select_n | solution.py:47
  465.4 278.4 %all_to_all.56 = bf16[1,512,32,768]{3,2,0,1:T(8,128)(2,1)S(1)} all-to-all(bf16[1,512,32,768]{3,2,0,1:T(8,128)(2,1)} %fusion.3), channel_id=1, replica_groups=mesh['lat'=8,'lev'=4] {'lat'}, dimensions={1} | all-to-all | bytes 50331648 | tf_op jit(solution)/shard_map/all_to_all | solution.py:50
  743.8 8.7 copy.34
  752.5 23.2 %copy.35 = bf16[1,64,256,768]{3,1,0,2:T(8,128)(2,1)S(1)} copy(bf16[1,64,256,768]{3,2,1,0:T(8,128)(2,1)} %bitcast.83) | data formatting | bytes 50331648 | tf_op jit(solution)/shard_map/all_to_all | solution.py:50
  775.8 548.1 %all_to_all.57 = bf16[1,64,256,768]{3,1,0,2:T(8,128)(2,1)} all-to-all(bf16[1,64,256,768]{3,1,0,2:T(8,128)(2,1)S(1)} %copy.35), channel_id=1, replica_groups=mesh['lat'=8,'lev'=4] {'lev'}, dimensions={2} | all-to-all | bytes 50331648 | tf_op jit(solution)/shard_map/all_to_all | solution.py:49
  1323.9 23.9 %copy.36 = bf16[1,64,256,768]{3,2,1,0:T(8,128)(2,1)} copy(bf16[1,64,256,768]{3,1,0,2:T(8,128)(2,1)} %all_to_all.57) | data formatting | bytes 50331648 | tf_op jit(solution)/shard_map/all_to_all | solution.py:49
  1347.7 44.6 %copy.37 = bf16[4,1,64,64,768]{3,4,0,2,1:T(8,128)(2,1)} copy(bf16[4,1,64,64,768]{4,3,0,2,1:T(8,128)(2,1)} %bitcast.84) | data formatting | bytes 50331648 | tf_op jit(solution)/shard_map/all_to_all | solution.py:49
  1392.3 50.2 %convolution_bitcast_fusion = f32[64,4,32,4,32]{4,2,3,1,0:T(8,128)} fusion(bf16[4,64,64,24,32,1]{2,4,3,5,0,1:T(8,128)(2,1)} %bitcast.85, bf16[4,64,64,24,32,1]{2,4,3,0,5,1:T(8,128)(2,1)} %bitcast.86), kind=kOutput, calls=%fused_computation.10 | convolution fusion | flops 3221225472 | bytes 54525952 | tf_op jit(solution)/shard_map/esaql,fsaqk->selfk/dot_general | solution.py:58
  1442.5 14.7 copy.38
  1459.8 140.9 %reduce-scatter.2.cloned.1.call-done = f32[64,32,128]{0,2,1:T(8,128)} async-done(((f32[64,128,128]{0,2,1:T(8,128)}), f32[64,32,128]{0,2,1:T(8,128)}) %reduce-scatter.2.cloned.1.call-update) | async-done | bytes 1048592 | tf_op jit(solution)/shard_map/reduce_scatter | solution.py:62
  (39 shorter events, 20.6 us)
Async XLA Ops:
  13.1 202.8 %all-to-all-start.1 = ((bf16[32,256,256]{2,0,1:T(8,128)(2,1)}), bf16[32,256,256]{2,0,1:T(8,128)(2,1)}, u32[]{:S(2)}, u32[]{:S(2)}) async-start(bf16[32,256,256]{2,0,1:T(8,128)(2,1)} %copy.29), calls=%async_computation.1 | async-start | bytes 8388608 | tf_op jit(solution)/shard_map/all_to_all | solution.py:33
  199.9 10.8 copy-start.1
  200.0 12.1 copy-start
  215.9 5.6 copy-start.2
  215.9 144.5 %all-to-all-start = ((bf16[8,32,32,768]{3,2,1,0:T(8,128)(2,1)}), bf16[8,32,32,768]{3,2,1,0:T(8,128)(2,1)}, u32[]{:S(2)}, u32[]{:S(2)}) async-start(bf16[8,32,32,768]{3,2,1,0:T(8,128)(2,1)} %bitcast_dynamic-update-slice_fusion), calls=%async_computation | async-start | bytes 25165824 | tf_op jit(solution)/shard_map/all_to_all | solution.py:28
  221.4 1379.3 %reduce-scatter.2.cloned.1.call-start = ((), (), s32[]{:S(2)}) async-start(), calls=%async_computation.5 | async-start | bytes 10485760 | tf_op jit(solution)/shard_map/reduce_scatter | solution.py:62
  221.7 0.5 copy-start.4
  1442.5 14.7 copy-start.5
  1442.5 15.3 copy-start.3
Sparse Core Ops, SparseCore 0:
  1457.3 143.3 reduce-scatter.1
